TPU v7x, 256 devices: a whole 4x4x8 slice. The times are simulated.
256 devices in a mesh: rp: 8 (over x, z_lo), pb: 32 (over z_hi, y, core).
Axes of the slice: x: 4, y: 4, z: 8 (z_hi: 4, z_lo: 2; z = z_hi * 2 + z_lo), core: 2. Of those that a mesh axis runs over, the one named last changes fastest.
Arguments:
- wannier_g: bfloat16 [2, 1024, 32, 1152], P(None, 'rp', 'pb'), may hold values from -0.19921875 to 0.19921875
- rp_coords: int32 [3, 1024], replicated, may hold values from -8 to 8
- q_coords: int32 [3, 512], P(None, ('rp', 'pb')), may hold values from 0 to 15
- k_index: int32 [1], replicated, may hold values from 0 to 7
- k_vectors: bfloat16 [8, 2, 32, 32], replicated, may hold values from -0.75 to 0.75
- kq_vectors: bfloat16 [512, 2, 32, 32], P(('rp', 'pb')), may hold values from -0.75 to 0.75
- modes: bfloat16 [512, 2, 36, 36], P(('rp', 'pb')), may hold values from -0.75 to 0.75
Outputs:
- rotated: float32 [512, 2, 32, 1152], P(('rp', 'pb'))
All inputs are finite; a program needn't handle non-finite values.
Results may differ from a plain program's by a relative error of at most 0.0054.
Values may be sent and summed in bfloat16 or wider, within the bound.
A program may use at most 64 MiB of HBM per device.

v0:
```python
import math
import jax
import jax.numpy as jnp
from jax import lax
from jax.sharding import PartitionSpec as P

NK = 16


def in_blocks(x, dim, length):
    shape = x.shape
    parts = x.reshape(*shape[:dim], length, shape[dim] // length, *shape[dim + 1 :])
    return jnp.moveaxis(parts, dim, 0)


def joined_along(parts, dim):
    shape = list(parts.shape[1:])
    shape[dim] *= parts.shape[0]
    return jnp.moveaxis(parts, 0, dim).reshape(shape)


def one_exchange(x, axis, axes, splits, concats):
    sizes = [lax.axis_size(a) for a in axes]
    parts = in_blocks(x, splits[0], sizes[0])
    parts = jnp.moveaxis(in_blocks(parts, splits[1] + 1, sizes[1]), 0, 1)
    inside = parts.shape[2:]
    parts = parts.reshape(-1, *inside)
    parts = lax.all_to_all(parts, axis, split_axis=0, concat_axis=0, tiled=True)
    parts = joined_along(parts.reshape(*sizes, *inside), concats[0] + 1)
    return joined_along(parts, concats[1])


def phases(q_rows, r_coords):
    turns = jnp.mod(jnp.sum(q_rows[:, :, None] * r_coords[:, None, :], axis=0), NK)
    angle = turns.astype(jnp.float32) * (2.0 * math.pi / NK)
    cosine = jnp.cos(angle).astype(jnp.bfloat16)
    sine = jnp.sin(angle).astype(jnp.bfloat16)
    return (jnp.concatenate([cosine, -sine], axis=1), jnp.concatenate([sine, cosine], axis=1))


def rotate(fourier, mode_vecs, unit, kq_vecs):
    count = fourier.shape[0]
    bands = kq_vecs.shape[2]
    branches = mode_vecs.shape[2]
    field = fourier.reshape(count, 2, bands, bands, branches)
    e_real, e_imag = (mode_vecs[:, 0], mode_vecs[:, 1])
    e_block = jnp.stack([jnp.stack([e_real, e_imag], 2), jnp.stack([-e_imag, e_real], 2)], 1)
    by_mode = jnp.einsum(
        "qcmnv,qcvdu->qdmnu", field, e_block, preferred_element_type=jnp.float32
    ).astype(jnp.bfloat16)
    u_real, u_imag = (unit[0], unit[1])
    u_block = jnp.stack([jnp.stack([u_real, u_imag], 1), jnp.stack([-u_imag, u_real], 1)], 0)
    by_band = jnp.einsum(
        "qcmnu,cndj->qdmju", by_mode, u_block, preferred_element_type=jnp.float32
    ).astype(jnp.bfloat16)
    v_real, v_imag = (kq_vecs[:, 0], kq_vecs[:, 1])
    v_block = jnp.stack([jnp.stack([v_real, -v_imag], 2), jnp.stack([v_imag, v_real], 2)], 1)
    result = jnp.einsum("qcmju,qcmdi->qdiju", by_band, v_block, preferred_element_type=jnp.float32)
    return result.reshape(count, 2, bands, bands * branches)


def local(wannier_g, rp_coords, q_coords, k_index, k_vectors, kq_vectors, modes):
    q_all = lax.all_gather(q_coords, ("rp", "pb"), axis=1, tiled=True)
    total = q_all.shape[1]
    groups = lax.axis_size("rp")
    block = total // groups
    moved = lax.all_to_all(wannier_g, "rp", split_axis=3, concat_axis=1, tiled=True)
    right = moved.reshape(2 * moved.shape[1], -1)
    q_blocks = q_all.reshape(3, groups, block).transpose(1, 0, 2)

    def fourier_block(q_rows):
        left_real, left_imag = phases(q_rows, rp_coords)
        f_real = jnp.dot(left_real, right, preferred_element_type=jnp.float32).astype(jnp.bfloat16)
        f_imag = jnp.dot(left_imag, right, preferred_element_type=jnp.float32).astype(jnp.bfloat16)
        return jnp.stack([f_real, f_imag], 1)

    fourier = lax.map(fourier_block, q_blocks).reshape(total, 2, moved.shape[2], moved.shape[3])
    owned = one_exchange(fourier, ("rp", "pb"), ("rp", "pb"), (0, 0), (3, 2))
    select = (jnp.arange(k_vectors.shape[0]) == k_index[0]).astype(jnp.bfloat16)
    unit = jnp.einsum("k,kcnj->cnj", select, k_vectors, preferred_element_type=jnp.float32).astype(
        jnp.bfloat16
    )
    return rotate(owned, modes, unit, kq_vectors)


def solution(mesh):
    return jax.shard_map(
        local,
        mesh=mesh,
        in_specs=(
            P(None, "rp", "pb", None),
            P(),
            P(None, ("rp", "pb")),
            P(),
            P(),
            P(("rp", "pb"), None, None, None),
            P(("rp", "pb"), None, None, None),
        ),
        out_specs=P(("rp", "pb"), None, None, None),
        check_vma=False,
    )
```

profile of v0, /device:TPU:1, one launch (start us, length us, event | category | flops | bytes accessed | tf_op | source)
XLA Modules:
  0.0 424.2 jit_solution(9630580377085636037)
XLA Ops:
  0.0 3.0 copy.101
  3.0 6.2 %all-to-all-start = ((bf16[2,128,1,1152]{1,0,2,3:T(2,128)(2,1)}), bf16[2,128,1,1152]{1,0,2,3:T(2,128)(2,1)S(1)}, u32[]{:S(2)}, u32[]{:S(2)}) async-start(bf16[2,128,1,1152]{1,0,2,3:T(2,128)(2,1)} %copy.101), calls=%async_computation | async-start | bytes 1179648 | tf_op jit(solution)/shard_map/all_to_all | solution.py:67
  9.9 0.2 fusion.19
  10.3 350.8 %all-gather = s32[256,2,3]{2,1,0:T(2,128)S(1)} all-gather(s32[1,2,3]{2,1,0:T(2,128)S(1)} %bitcast.145), channel_id=1, replica_groups=mesh['rp'=8,'pb'=32] {'rp','pb'}, dimensions={0}, use_global_device_ids=true | all-gather | bytes 6168 | tf_op jit(solution)/shard_map/all_gather | solution.py:63
  361.4 0.5 copy.128
  362.0 27.2 %while.12 = (s32[]{:T(128)}, bf16[8,64,2,144]{3,2,1,0:T(2,128)(2,1)}, s32[8,3,64]{2,0,1:T(8,128)S(1)}, s32[3,1024]{1,0:T(4,128)S(1)}, bf16[2048,144]{1,0:T(8,128)(2,1)S(1)}, /*index=5*/s32[]{:T(128)}) while((s32[]{:T(128)}, bf16[8,64,2,144]{3,2,1,0:T(2,128)(2,1)}, s32[8,3,64]{2,0,1:T(8,128)S(1)}, s32[3,1024]{1,0:T(4,128)S(1)}, ...), condition=%wide.region_2.3_spmd, body=%wide.region_0.2_spmd.sunk | while | flops 78942208 | bytes 3112789 | solution.py:77
  362.1 0.9 cosine_convert_fusion.2
  363.1 1.0 fusion.51
  364.1 0.3 fusion.52
  364.4 0.3 fusion.53
  364.7 0.7 copy_dynamic-update-slice_fusion.2
  365.4 0.1 multiply_reduce_fusion.2
  365.5 0.9 cosine_convert_fusion.2
  366.5 1.0 fusion.51
  367.4 0.3 fusion.52
  367.7 0.3 fusion.53
  368.1 0.7 copy_dynamic-update-slice_fusion.2
  368.8 0.1 multiply_reduce_fusion.2
  368.9 0.9 cosine_convert_fusion.2
  369.9 1.0 fusion.51
  370.8 0.3 fusion.52
  371.1 0.3 fusion.53
  371.5 0.7 copy_dynamic-update-slice_fusion.2
  372.2 0.1 multiply_reduce_fusion.2
  372.3 0.9 cosine_convert_fusion.2
  373.3 1.0 fusion.51
  374.2 0.3 fusion.52
  374.5 0.3 fusion.53
  374.9 0.7 copy_dynamic-update-slice_fusion.2
  375.6 0.1 multiply_reduce_fusion.2
  375.7 0.9 cosine_convert_fusion.2
  376.6 1.0 fusion.51
  377.6 0.3 fusion.52
  377.9 0.3 fusion.53
  378.2 0.7 copy_dynamic-update-slice_fusion.2
  378.9 0.1 multiply_reduce_fusion.2
  379.1 0.9 cosine_convert_fusion.2
  380.0 1.0 fusion.51
  381.0 0.3 fusion.52
  381.3 0.3 fusion.53
  381.6 0.7 copy_dynamic-update-slice_fusion.2
  382.3 0.1 multiply_reduce_fusion.2
  382.5 0.9 cosine_convert_fusion.2
  383.4 1.0 fusion.51
  384.4 0.3 fusion.52
  384.7 0.3 fusion.53
  385.0 0.7 copy_dynamic-update-slice_fusion.2
  385.7 0.1 multiply_reduce_fusion.2
  385.9 0.9 cosine_convert_fusion.2
  386.8 1.0 fusion.51
  387.8 0.3 fusion.52
  388.1 0.3 fusion.53
  388.4 0.7 copy_dynamic-update-slice_fusion.2
  389.1 5.3 %all-to-all-start.1 = ((bf16[256,2,2,1,144]{4,2,1,3,0:T(2,128)(2,1)}), bf16[256,2,2,1,144]{4,2,1,3,0:T(2,128)(2,1)S(1)}, u32[]{:S(2)}, u32[]{:S(2)}) async-start(bf16[256,2,2,1,144]{4,2,1,3,0:T(2,128)(2,1)} %bitcast.38), calls=%async_computation.1 | async-start | bytes 1048576 | tf_op jit(solution)/shard_map/all_to_all | solution.py:28
  394.8 0.1 maximum_bitcast_fusion.1
  394.9 20.4 %all-to-all-done.1 = bf16[256,2,2,1,144]{4,2,1,3,0:T(2,128)(2,1)S(1)} async-done(((bf16[256,2,2,1,144]{4,2,1,3,0:T(2,128)(2,1)}), bf16[256,2,2,1,144]{4,2,1,3,0:T(2,128)(2,1)S(1)}, u32[]{:S(2)}, u32[]{:S(2)}) %all-to-all-start.1) | async-done | bytes 294944 | tf_op jit(solution)/shard_map/all_to_all | solution.py:28
  415.4 0.3 copy.109
  415.7 0.5 reshape.52
  416.2 2.8 reshape_reshape.3
  419.0 0.5 fusion.13
  419.5 0.5 fusion.14
  420.0 0.5 convolution_bitcast_fusion
  420.5 1.2 copy.114
  421.7 2.4 reshape.53
  (54 shorter events, 1.2 us)
Async XLA Ops:
  0.0 9.9 %copy-start = (bf16[8,2,32,32]{3,2,1,0:T(8,128)(2,1)S(1)}, bf16[8,2,32,32]{3,2,1,0:T(8,128)(2,1)}, u32[]{:S(2)}) copy-start(bf16[8,2,32,32]{3,2,1,0:T(8,128)(2,1)} %param.13) | copy-start | bytes 98308
  0.0 10.2 %copy-start.3 = (bf16[2,2,32,32]{3,2,1,0:T(8,128)(2,1)S(1)}, bf16[2,2,32,32]{3,2,1,0:T(8,128)(2,1)}, u32[]{:S(2)}) copy-start(bf16[2,2,32,32]{3,2,1,0:T(8,128)(2,1)} %param.14) | copy-start | bytes 24580
  0.0 10.3 %copy-start.4 = (s32[3,2]{0,1:T(2,128)S(1)}, s32[3,2]{0,1:T(2,128)}, u32[]{:S(2)}) copy-start(s32[3,2]{0,1:T(2,128)} %param.11) | copy-start | bytes 76
  0.0 361.3 %copy-start.2 = (bf16[2,2,36,36]{3,1,2,0:T(2,128)(2,1)S(1)}, bf16[2,2,36,36]{3,1,2,0:T(2,128)(2,1)}, u32[]{:S(2)}) copy-start(bf16[2,2,36,36]{3,1,2,0:T(2,128)(2,1)} %param.15) | copy-start | bytes 31108
  3.0 358.3 %all-to-all-start = ((bf16[2,128,1,1152]{1,0,2,3:T(2,128)(2,1)}), bf16[2,128,1,1152]{1,0,2,3:T(2,128)(2,1)S(1)}, u32[]{:S(2)}, u32[]{:S(2)}) async-start(bf16[2,128,1,1152]{1,0,2,3:T(2,128)(2,1)} %copy.101), calls=%async_computation | async-start | bytes 1179648 | tf_op jit(solution)/shard_map/all_to_all | solution.py:67
  9.2 352.8 %copy-start.1 = (s32[3,1024]{1,0:T(4,128)S(1)}, s32[3,1024]{1,0:T(4,128)}, u32[]{:S(2)}) copy-start(s32[3,1024]{1,0:T(4,128)} %param.10) | copy-start | bytes 36868
  389.1 26.2 %all-to-all-start.1 = ((bf16[256,2,2,1,144]{4,2,1,3,0:T(2,128)(2,1)}), bf16[256,2,2,1,144]{4,2,1,3,0:T(2,128)(2,1)S(1)}, u32[]{:S(2)}, u32[]{:S(2)}) async-start(bf16[256,2,2,1,144]{4,2,1,3,0:T(2,128)(2,1)} %bitcast.38), calls=%async_computation.1 | async-start | bytes 1048576 | tf_op jit(solution)/shard_map/all_to_all | solution.py:28
where the time goes:
time: 424 us
  blocking collectives  351 us (83%)
  waiting for transfers between devices  20.4 us (5%)
  local copies, waits for them, and re-layouts  17 us (4%)
  other arithmetic  16.8 us (4%)
  starting transfers between devices  11.5 us (3%)
  matrix products  6.36 us (2%)
    all_gather x1, blocking collectives, local(): q_all = lax.all_gather(q_coords, ('rp', 'pb'), axis=1, tiled=True)  351 us
    all_to_all x1, waiting for transfers between devices, one_exchange(): parts = lax.all_to_all(parts, axis, split_axis=0, concat_axis=0, tiled=True)  20.4 us
  transfers between devices with their start and end apart: 2, of which 1 were waited for; matrix products, arithmetic and copies ran while one was open for 0% of the time, Pallas kernels for 0%

commit v1 on v0

--- a/solution.py
+++ b/solution.py
@@ -60,7 +60,10 @@
 
 
 def local(wannier_g, rp_coords, q_coords, k_index, k_vectors, kq_vectors, modes):
-    q_all = lax.all_gather(q_coords, ("rp", "pb"), axis=1, tiled=True)
+    q_all = jnp.concatenate(
+        lax.all_to_all(jnp.stack([q_coords] * lax.axis_size(("rp", "pb"))), ("rp", "pb"), 0, 0),
+        axis=1,
+    )
     total = q_all.shape[1]
     groups = lax.axis_size("rp")
     block = total // groups

time: 424 us -> 111 us (0.26)
  blocking collectives: 351 us -> 0 us
  waiting for transfers between devices: 20.4 us -> 42 us
  starting transfers between devices: 11.5 us -> 25.8 us
    all_gather x1 -> x0, blocking collectives: 351 us -> none  [local(): q_all = lax.all_gather(q_coords, ('rp', 'pb'), axis=1, tiled=True)]
    all_to_all x0 -> x1, starting transfers between devices: none -> 15.6 us  [local(): lax.all_to_all(jnp.stack([q_coords] * lax.axis_size(('rp', 'pb'))), ('rp'...]
    all_to_all x0 -> x1, waiting for transfers between devices: none -> 11.7 us  [local(): lax.all_to_all(jnp.stack([q_coords] * lax.axis_size(('rp', 'pb'))), ('rp'...]
    all_to_all x1, waiting for transfers between devices: 0.01 us -> 9.78 us  [local(): lax.all_to_all(wannier_g, 'rp', split_axis=3, concat_axis=1, tiled=True)]
  transfers between devices with their start and end apart: 2 -> 3, of which waited for: 1 -> 3; matrix products, arithmetic and copies ran while one was open for 0% -> 4% of each run, Pallas kernels for 0% -> 0%
where the time goes in v1:
time: 111 us
  waiting for transfers between devices  42 us (38%)
  starting transfers between devices  25.8 us (23%)
  local copies, waits for them, and re-layouts  18.4 us (17%)
  other arithmetic  16.8 us (15%)
  matrix products  6.36 us (6%)
    all_to_all x1, waiting for transfers between devices, one_exchange(): parts = lax.all_to_all(parts, axis, split_axis=0, concat_axis=0, tiled=True)  20.6 us
    all_to_all x1, starting transfers between devices, local(): lax.all_to_all(jnp.stack([q_coords] * lax.axis_size(('rp', 'pb'))), ('rp'...  15.6 us
    all_to_all x1, waiting for transfers between devices, local(): lax.all_to_all(jnp.stack([q_coords] * lax.axis_size(('rp', 'pb'))), ('rp'...  11.7 us
    all_to_all x1, waiting for transfers between devices, local(): lax.all_to_all(wannier_g, 'rp', split_axis=3, concat_axis=1, tiled=True)  9.78 us
    neg x8, other arithmetic, phases(): -sine  7.76 us
    convert_element_type x8, other arithmetic, phases(): cosine = jnp.cos(angle).astype(jnp.bfloat16)  7.6 us
    all_to_all x1, starting transfers between devices, one_exchange(): parts = lax.all_to_all(parts, axis, split_axis=0, concat_axis=0, tiled=True)  6.58 us
    dynamic_update_slice x8, local copies, waits for them, and re-layouts, local(): lax.map(fourier_block, q_blocks)  5.58 us
  transfers between devices with their start and end apart: 3, of which 3 were waited for; matrix products, arithmetic and copies ran while one was open for 4% of the time, Pallas kernels for 0%

profile of v1, /device:TPU:1, one launch (start us, length us, event | category | flops | bytes accessed | tf_op | source)
XLA Modules:
  0.0 110.6 jit_solution(1078761208489852443)
XLA Ops:
  0.0 1.5 %stack.62 = s32[256,3,2]{1,2,0:T(2,128)} broadcast(s32[3,2]{0,1:T(2,128)} %param.11), dimensions={1,2} | broadcast | bytes 6168 | tf_op jit(solution)/shard_map/stack | solution.py:64
  1.5 15.6 %all-to-all-start = ((s32[256,3,2]{1,2,0:T(2,128)}), s32[256,3,2]{1,2,0:T(2,128)S(1)}, u32[]{:S(2)}, u32[]{:S(2)}) async-start(s32[256,3,2]{1,2,0:T(2,128)} %stack.62), calls=%async_computation | async-start | bytes 524288 | tf_op jit(solution)/shard_map/all_to_all | solution.py:64
  17.8 0.2 fusion.19
  18.1 2.9 %copy.102 = bf16[2,128,1,1152]{1,0,2,3:T(2,128)(2,1)} copy(bf16[2,128,1,1152]{3,1,2,0:T(8,128)(2,1)} %param.9) | data formatting | bytes 1179648 | tf_op args[0]
  21.1 11.7 %all-to-all-done = s32[256,3,2]{1,2,0:T(2,128)S(1)} async-done(((s32[256,3,2]{1,2,0:T(2,128)}), s32[256,3,2]{1,2,0:T(2,128)S(1)}, u32[]{:S(2)}, u32[]{:S(2)}) %all-to-all-start) | async-done | bytes 6176 | tf_op jit(solution)/shard_map/all_to_all | solution.py:64
  32.7 3.5 %all-to-all-start.1 = ((bf16[2,128,1,1152]{1,0,2,3:T(2,128)(2,1)}), bf16[2,128,1,1152]{1,0,2,3:T(2,128)(2,1)S(1)}, u32[]{:S(2)}, u32[]{:S(2)}) async-start(bf16[2,128,1,1152]{1,0,2,3:T(2,128)(2,1)} %copy.102), calls=%async_computation.1 | async-start | bytes 1179648 | tf_op jit(solution)/shard_map/all_to_all | solution.py:70
  36.5 0.1 copy.105
  36.6 9.8 %all-to-all-done.1 = bf16[2,128,1,1152]{1,0,2,3:T(2,128)(2,1)S(1)} async-done(((bf16[2,128,1,1152]{1,0,2,3:T(2,128)(2,1)}), bf16[2,128,1,1152]{1,0,2,3:T(2,128)(2,1)S(1)}, u32[]{:S(2)}, u32[]{:S(2)}) %all-to-all-start.1) | async-done | bytes 589856 | tf_op jit(solution)/shard_map/all_to_all | solution.py:70
  46.5 0.5 copy.131
  47.0 27.1 %while.12 = (s32[]{:T(128)}, bf16[8,64,2,144]{3,2,1,0:T(2,128)(2,1)}, s32[8,3,64]{2,1,0:T(4,128)S(1)}, s32[3,1024]{1,0:T(4,128)S(1)}, bf16[2048,144]{1,0:T(8,128)(2,1)S(1)}, /*index=5*/s32[]{:T(128)}) while((s32[]{:T(128)}, bf16[8,64,2,144]{3,2,1,0:T(2,128)(2,1)}, s32[8,3,64]{2,1,0:T(4,128)S(1)}, s32[3,1024]{1,0:T(4,128)S(1)}, ...), condition=%wide.region_2.3_spmd, body=%wide.region_0.2_spmd.sunk | while | flops 78942208 | bytes 3111253 | solution.py:80
  47.2 0.9 cosine_convert_fusion.2
  48.1 1.0 fusion.51
  49.1 0.3 fusion.52
  49.4 0.3 fusion.53
  49.7 0.7 copy_dynamic-update-slice_fusion.2
  50.4 0.1 multiply_reduce_fusion.2
  50.5 0.9 cosine_convert_fusion.2
  51.5 1.0 fusion.51
  52.5 0.3 fusion.52
  52.8 0.3 fusion.53
  53.1 0.7 copy_dynamic-update-slice_fusion.2
  53.8 0.1 multiply_reduce_fusion.2
  53.9 0.9 cosine_convert_fusion.2
  54.9 1.0 fusion.51
  55.8 0.3 fusion.52
  56.1 0.3 fusion.53
  56.5 0.7 copy_dynamic-update-slice_fusion.2
  57.2 0.1 multiply_reduce_fusion.2
  57.3 0.9 cosine_convert_fusion.2
  58.3 1.0 fusion.51
  59.2 0.3 fusion.52
  59.5 0.3 fusion.53
  59.9 0.7 copy_dynamic-update-slice_fusion.2
  60.7 0.9 cosine_convert_fusion.2
  61.6 1.0 fusion.51
  62.6 0.3 fusion.52
  62.9 0.3 fusion.53
  63.2 0.7 copy_dynamic-update-slice_fusion.2
  64.1 0.9 cosine_convert_fusion.2
  65.0 1.0 fusion.51
  66.0 0.3 fusion.52
  66.3 0.3 fusion.53
  66.6 0.7 copy_dynamic-update-slice_fusion.2
  67.5 0.9 cosine_convert_fusion.2
  68.4 1.0 fusion.51
  69.4 0.3 fusion.52
  69.7 0.3 fusion.53
  70.0 0.7 copy_dynamic-update-slice_fusion.2
  70.9 0.9 cosine_convert_fusion.2
  71.8 1.0 fusion.51
  72.8 0.3 fusion.52
  73.1 0.3 fusion.53
  73.4 0.7 copy_dynamic-update-slice_fusion.2
  74.1 6.6 %all-to-all-start.2 = ((bf16[256,2,2,1,144]{4,2,1,3,0:T(2,128)(2,1)}), bf16[256,2,2,1,144]{4,2,1,3,0:T(2,128)(2,1)S(1)}, u32[]{:S(2)}, u32[]{:S(2)}) async-start(bf16[256,2,2,1,144]{4,2,1,3,0:T(2,128)(2,1)} %bitcast.37), calls=%async_computation.2 | async-start | bytes 1048576 | tf_op jit(solution)/shard_map/all_to_all | solution.py:28
  81.0 0.1 maximum_bitcast_fusion.1
  81.2 20.6 %all-to-all-done.2 = bf16[256,2,2,1,144]{4,2,1,3,0:T(2,128)(2,1)S(1)} async-done(((bf16[256,2,2,1,144]{4,2,1,3,0:T(2,128)(2,1)}), bf16[256,2,2,1,144]{4,2,1,3,0:T(2,128)(2,1)S(1)}, u32[]{:S(2)}, u32[]{:S(2)}) %all-to-all-start.2) | async-done | bytes 294944 | tf_op jit(solution)/shard_map/all_to_all | solution.py:28
  101.8 0.3 copy.110
  102.1 0.5 reshape.54
  102.6 2.8 %reshape_reshape.7 = bf16[2,2,32,32,36]{4,3,2,1,0:T(8,128)(2,1)S(1)} reshape(bf16[2,2,32,1,1152]{4,2,1,0,3:T(8,128)(2,1)S(1)} %bitcast.134) | data formatting | bytes 589824 | tf_op jit(solution)/shard_map/reshape;reshape | solution.py:45
  105.4 0.5 fusion.13
  105.9 0.5 fusion.14
  106.4 0.5 convolution_bitcast_fusion
  106.9 1.2 %copy.115 = f32[2,2,32,32,36]{4,3,2,1,0:T(8,128)S(1)} copy(f32[2,2,32,32,36]{4,2,3,1,0:T(8,128)S(1)} %convolution_bitcast_fusion) | data formatting | bytes 1179648 | tf_op jit(solution)/shard_map/qcmju,qcmdi->qdiju/dot_general | solution.py:58
  108.1 2.4 %reshape.55 = f32[2,2,32,1152]{3,2,1,0:T(8,128)} reshape(f32[2,2,32,32,36]{4,3,2,1,0:T(8,128)S(1)} %copy.115) | data formatting | bytes 1179648 | tf_op jit(solution)/shard_map/reshape | solution.py:59
  (45 shorter events, 1.5 us)
Async XLA Ops:
  0.0 17.8 %copy-start = (bf16[8,2,32,32]{3,2,1,0:T(8,128)(2,1)S(1)}, bf16[8,2,32,32]{3,2,1,0:T(8,128)(2,1)}, u32[]{:S(2)}) copy-start(bf16[8,2,32,32]{3,2,1,0:T(8,128)(2,1)} %param.13) | copy-start | bytes 98308
  0.0 36.3 %copy-start.3 = (bf16[2,2,32,32]{3,2,1,0:T(8,128)(2,1)S(1)}, bf16[2,2,32,32]{3,2,1,0:T(8,128)(2,1)}, u32[]{:S(2)}) copy-start(bf16[2,2,32,32]{3,2,1,0:T(8,128)(2,1)} %param.14) | copy-start | bytes 24580
  0.0 36.4 %copy-start.2 = (bf16[2,2,36,36]{3,1,2,0:T(2,128)(2,1)S(1)}, bf16[2,2,36,36]{3,1,2,0:T(2,128)(2,1)}, u32[]{:S(2)}) copy-start(bf16[2,2,36,36]{3,1,2,0:T(2,128)(2,1)} %param.15) | copy-start | bytes 31108
  1.5 31.2 %all-to-all-start = ((s32[256,3,2]{1,2,0:T(2,128)}), s32[256,3,2]{1,2,0:T(2,128)S(1)}, u32[]{:S(2)}, u32[]{:S(2)}) async-start(s32[256,3,2]{1,2,0:T(2,128)} %stack.62), calls=%async_computation | async-start | bytes 524288 | tf_op jit(solution)/shard_map/all_to_all | solution.py:64
  21.1 25.9 %copy-start.1 = (s32[3,1024]{1,0:T(4,128)S(1)}, s32[3,1024]{1,0:T(4,128)}, u32[]{:S(2)}) copy-start(s32[3,1024]{1,0:T(4,128)} %param.10) | copy-start | bytes 36868
  32.7 13.7 %all-to-all-start.1 = ((bf16[2,128,1,1152]{1,0,2,3:T(2,128)(2,1)}), bf16[2,128,1,1152]{1,0,2,3:T(2,128)(2,1)S(1)}, u32[]{:S(2)}, u32[]{:S(2)}) async-start(bf16[2,128,1,1152]{1,0,2,3:T(2,128)(2,1)} %copy.102), calls=%async_computation.1 | async-start | bytes 1179648 | tf_op jit(solution)/shard_map/all_to_all | solution.py:70
  74.1 27.6 %all-to-all-start.2 = ((bf16[256,2,2,1,144]{4,2,1,3,0:T(2,128)(2,1)}), bf16[256,2,2,1,144]{4,2,1,3,0:T(2,128)(2,1)S(1)}, u32[]{:S(2)}, u32[]{:S(2)}) async-start(bf16[256,2,2,1,144]{4,2,1,3,0:T(2,128)(2,1)} %bitcast.37), calls=%async_computation.2 | async-start | bytes 1048576 | tf_op jit(solution)/shard_map/all_to_all | solution.py:28
